TPU v7x, 32 devices: a whole 2x2x4 slice. The times are simulated.
32 devices in a mesh: seq: 4 (over z), wt: 8 (over y, x, core).
Axes of the slice: x: 2, y: 2, z: 4, core: 2. Of those that a mesh axis runs over, the one named last changes fastest.
Arguments:
- tokens: bfloat16 [8, 512, 2048], P('wt', 'seq'), may hold values from -6 to 6
- cotangent: bfloat16 [8, 512, 2048], P('wt', 'seq'), may hold values from -6 to 6
- segment_ids: int32 [8, 512], P('wt'), may hold values from 0 to 1, never falling along the last dimension, each value on 1 to 320 neighbouring positions
- expert_routes: int32 [8, 512, 8], P('wt', 'seq'), may hold values from 0 to 15, all different within a row; in each aligned block of 128 rows (0 to 127, 128 to 255, ..., all dimensions but the last counted through in order) at most 128 rows name the same one
- w_qkv: bfloat16 [2048, 6144], P('wt'), may hold values from -0.125 to 0.125
- w_out: bfloat16 [2048, 2048], P('wt'), may hold values from -2 to 2
- w_router: bfloat16 [2048, 16], P('wt'), may hold values from -0.0625 to 0.0625
- w_gate_up: bfloat16 [16, 2048, 2048], P('seq', 'wt'), may hold values from -0.125 to 0.125
- w_down: bfloat16 [16, 1024, 2048], P('seq', 'wt'), may hold values from -0.75 to 0.75
- attn_gain: bfloat16 [2048], P('wt'), may hold values from 0.5 to 1.5
- ffn_gain: bfloat16 [2048], P('wt'), may hold values from 0.5 to 1.5
- q_gain: bfloat16 [128], P('wt'), may hold values from 0.5 to 1.5
- k_gain: bfloat16 [128], P('wt'), may hold values from 0.5 to 1.5
Outputs:
- output: bfloat16 [8, 512, 2048], P('wt', 'seq')
- tokens_grad: float32 [8, 512, 2048], P('wt', 'seq')
- w_qkv_grad: float32 [2048, 6144], P('wt')
- w_out_grad: float32 [2048, 2048], P('wt')
- w_router_grad: float32 [2048, 16], P('wt')
- w_gate_up_grad: float32 [16, 2048, 2048], P('seq', 'wt')
- w_down_grad: float32 [16, 1024, 2048], P('seq', 'wt')
- attn_gain_grad: float32 [2048], P('wt')
- ffn_gain_grad: float32 [2048], P('wt')
- q_gain_grad: float32 [128], P('wt')
- k_gain_grad: float32 [128], P('wt')
Inputs may be any that keep to these rules, and one draw needn't show every extreme that they name: `segment_ids`: along a sequence the segment numbers never fall; each of the 2 documents spans 1 to 320 positions. `expert_routes`: A token names 8 different experts; among the 128 tokens of one device no expert is named more than 128 times, a bound that some block reaches.
All inputs are finite; a program needn't handle non-finite values.
Results may differ from a plain program's by a relative error of at most 0.028.
Values may be sent and summed in bfloat16 or wider, within the bound.
A program may use at most 512 MiB of HBM per device.

v0:
```python
import jax
import jax.numpy as jnp
import numpy as np
from jax import lax
from jax.sharding import PartitionSpec as P

H = 16
HD = 128
FF = 1024
EPS = 1e-06
THETA = 50000.0
NEG = -1e30
LANES = 128
BF = jnp.bfloat16
F32 = jnp.float32


def normalize(values):
    factor = lax.rsqrt(jnp.mean(values * values, axis=-1, keepdims=True) + EPS)
    return (values * factor, factor)


def norm_back(grad_normed, normed_values, factor):
    return factor * (
        grad_normed - normed_values * jnp.mean(grad_normed * normed_values, axis=-1, keepdims=True)
    )


def rope_tables(length):
    half = HD // 2
    freq = THETA ** (-jnp.arange(half, dtype=F32) * 2.0 / HD)
    angle = jnp.arange(length, dtype=F32)[:, None] * freq[None, :]
    return (jnp.cos(angle)[:, None, :], jnp.sin(angle)[:, None, :])


def rotate(values, cosine, sine):
    half = values.shape[-1] // 2
    first = values[..., :half]
    second = values[..., half:]
    return jnp.concatenate(
        [first * cosine - second * sine, second * cosine + first * sine], axis=-1
    )


def dot(left, right, dims):
    return lax.dot_general(left, right, (dims, ((), ())), preferred_element_type=F32)


def nn(left, right):
    return dot(left, right, ((1,), (0,)))


def nt(left, right):
    return dot(left, right, ((1,), (1,)))


def tn(left, right):
    return dot(left, right, ((0,), (0,)))


def split_two(values):
    high = values.astype(BF)
    low = (values - high.astype(F32)).astype(BF)
    return (high, low)


def body(
    tokens,
    cotangent,
    segment_ids,
    expert_routes,
    w_qkv,
    w_out,
    w_router,
    w_gate_up,
    w_down,
    attn_gain,
    ffn_gain,
    q_gain,
    k_gain,
):
    seq_total = lax.axis_size("seq")
    wt_total = lax.axis_size("wt")
    seq_me = lax.axis_index("seq")
    rows = tokens.shape[1]
    model = tokens.shape[2]
    length = rows * seq_total
    shard = w_qkv.shape[0]
    local_experts = w_gate_up.shape[0]
    experts = w_router.shape[1]
    heads = H // seq_total
    cols = 3 * heads * HD
    gain_part = q_gain.shape[0]
    tokens_all = lax.all_gather(tokens[0], "seq", axis=0, tiled=True)
    routes_all = lax.all_gather(expert_routes[0], "seq", axis=0, tiled=True)
    w_here = lax.dynamic_slice_in_dim(
        w_qkv.reshape(shard, 3, seq_total, heads * HD), seq_me, 1, axis=2
    ).reshape(shard, cols)
    small = jnp.concatenate(
        [
            w_router,
            attn_gain[:, None],
            ffn_gain[:, None],
            jnp.pad(q_gain, (0, shard - gain_part))[:, None],
            jnp.pad(k_gain, (0, shard - gain_part))[:, None],
        ],
        axis=1,
    )
    small = jnp.pad(small, ((0, 0), (0, LANES - small.shape[1])))
    qkv_full = lax.all_gather(jnp.concatenate([w_here, small], axis=1), "wt", axis=0, tiled=True)
    out_full = lax.all_gather(w_out, "wt", axis=0, tiled=True)
    grad_all = lax.all_gather(cotangent[0], "seq", axis=0, tiled=True)
    expert_full = [
        lax.all_gather(jnp.concatenate([w_gate_up[e], w_down[e]], axis=0), "wt", axis=0)
        for e in range(local_experts)
    ]
    small_full = qkv_full[:, cols:]
    router_full = small_full[:, :experts]
    picker = np.zeros((8, LANES), np.float32)
    for row in range(4):
        picker[row, experts + row] = 1.0
    gain_rows = nt(jnp.asarray(picker, BF), small_full)
    gain_attn = gain_rows[0]
    gain_ffn = gain_rows[1]
    gain_query = gain_rows[2].reshape(wt_total, shard)[:, :gain_part].reshape(HD)
    gain_key = gain_rows[3].reshape(wt_total, shard)[:, :gain_part].reshape(HD)
    segments = segment_ids[0]
    same = segments[:, None] == segments[None, :]
    cosine, sine = rope_tables(length)
    normed_all, _ = normalize(tokens_all.astype(F32))
    hidden = (normed_all * gain_attn).astype(BF)
    projected = nn(hidden, qkv_full)[:, :cols].reshape(length, 3, heads, HD)
    normed_q, factor_q = normalize(projected[:, 0])
    normed_k, factor_k = normalize(projected[:, 1])
    queries = jnp.swapaxes(rotate(normed_q * gain_query, cosine, sine).astype(BF), 0, 1)
    keys = jnp.swapaxes(rotate(normed_k * gain_key, cosine, sine).astype(BF), 0, 1)
    values = jnp.swapaxes(projected[:, 2].astype(BF), 0, 1)
    scale = HD ** (-0.5)

    def bmm(left, right, dims):
        return lax.dot_general(left, right, (dims, ((0,), (0,))), preferred_element_type=F32)

    logits = jnp.where(same[None], bmm(queries, keys, ((2,), (2,))) * scale, NEG)
    powers = jnp.exp(logits - jnp.max(logits, axis=-1, keepdims=True))
    weights = powers / jnp.sum(powers, axis=-1, keepdims=True)
    weights_low = weights.astype(BF)
    attended = bmm(weights_low, values, ((2,), (1,))).astype(BF)
    merged = lax.all_to_all(
        jnp.swapaxes(attended, 0, 1), "seq", split_axis=0, concat_axis=1, tiled=True
    ).reshape(rows, H * HD)
    inputs = tokens[0].astype(F32)
    residual = inputs + nn(merged, out_full)
    normed_f, factor_f = normalize(residual)
    hidden_own = (normed_f * gain_ffn).astype(BF)
    hidden_ffn = lax.all_gather(hidden_own, "seq", axis=0, tiled=True)
    chances = jax.nn.softmax(nn(hidden_ffn, router_full), axis=-1)
    expert_ids = jnp.arange(experts, dtype=jnp.int32)
    routed = jnp.any(routes_all[:, :, None] == expert_ids[None, None, :], axis=1)
    picked = jnp.where(routed, chances, 0.0)
    picked_total = jnp.sum(picked, axis=1, keepdims=True)
    gates = picked / picked_total
    gates_here = lax.dynamic_slice_in_dim(gates, seq_me * local_experts, local_experts, axis=1)
    out_part = jnp.zeros((length, model), F32)
    grad_hidden_part = jnp.zeros((length, model), F32)
    gate_grads = []
    expert_grads = []
    for e in range(local_experts):
        gate = gates_here[:, e : e + 1]
        gate_up = expert_full[e][:, : model // wt_total].reshape(model, 2 * FF)
        down = expert_full[e][:, model // wt_total :].reshape(FF, model)
        before = nn(hidden_ffn, gate_up)
        gate_part = before[:, :FF]
        up_part = before[:, FF:]
        sigmoid_gate = jax.nn.sigmoid(gate_part)
        silu_gate = gate_part * sigmoid_gate
        activated = silu_gate * up_part
        scaled = (gate * activated).astype(BF)
        grad_act = nt(grad_all, down)
        gate_grads.append(jnp.sum(grad_act * activated, axis=1, keepdims=True))
        grad_act = grad_act * gate
        grad_gate = grad_act * up_part * sigmoid_gate * (1.0 + gate_part * (1.0 - sigmoid_gate))
        grad_up = grad_act * silu_gate
        grad_before = jnp.concatenate([grad_gate, grad_up], axis=-1).astype(BF)
        out_part = out_part + nn(scaled, down)
        grad_hidden_part = grad_hidden_part + nt(grad_before, gate_up)
        gate_up_grad = tn(hidden_ffn, grad_before).astype(BF)
        down_grad = tn(scaled, grad_all).astype(BF)
        joined = jnp.concatenate(
            [
                gate_up_grad.reshape(wt_total, model // wt_total, 2 * FF),
                down_grad.reshape(wt_total, FF // wt_total, model),
            ],
            axis=1,
        )
        expert_grads.append(
            lax.psum_scatter(joined, "wt", scatter_dimension=0, tiled=False).astype(F32)
        )
    gate_up_out = jnp.stack([g[: model // wt_total] for g in expert_grads])
    down_out = jnp.stack([g[model // wt_total :] for g in expert_grads])
    gate_grad_part = jnp.concatenate(gate_grads, axis=1)
    gate_high, gate_low = split_two(gate_grad_part)

    def spread(part):
        wide = jnp.zeros((length, experts), BF)
        return lax.dynamic_update_slice(wide, part, (0, seq_me * local_experts))

    returned = lax.psum_scatter(
        jnp.concatenate([grad_hidden_part.astype(BF), spread(gate_high), spread(gate_low)], axis=1),
        "seq",
        scatter_dimension=0,
        tiled=True,
    ).astype(F32)
    grad_hidden = returned[:, :model]
    gate_grad = returned[:, model : model + experts] + returned[:, model + experts :]
    moe_out = lax.psum_scatter(out_part.astype(BF), "seq", scatter_dimension=0, tiled=True).astype(
        F32
    )
    output = (residual + moe_out).astype(BF)

    def own(full):
        return lax.dynamic_slice_in_dim(full, seq_me * rows, rows, axis=0)

    chances_own = own(chances)
    routed_own = own(routed)
    gates_own = own(gates)
    inner_gate = jnp.sum(gate_grad * gates_own, axis=1, keepdims=True)
    grad_chances = jnp.where(routed_own, (gate_grad - inner_gate) / own(picked_total), 0.0)
    grad_logits = (
        chances_own * (grad_chances - jnp.sum(grad_chances * chances_own, axis=1, keepdims=True))
    ).astype(BF)
    grad_hidden = grad_hidden + nt(grad_logits, router_full)
    router_grad = tn(hidden_own, grad_logits)
    ffn_gain_grad = jnp.sum(grad_hidden * normed_f, axis=0)
    grad_residual = cotangent[0].astype(F32) + norm_back(grad_hidden * gain_ffn, normed_f, factor_f)
    grad_branch = grad_residual.astype(BF)
    grad_merged = nt(grad_branch, out_full).astype(BF).reshape(rows, H, HD)
    grad_heads = jnp.swapaxes(
        lax.all_to_all(grad_merged, "seq", split_axis=1, concat_axis=0, tiled=True), 0, 1
    )
    out_grad = lax.psum_scatter(
        tn(merged, grad_branch).astype(BF), "wt", scatter_dimension=0, tiled=True
    )
    out_grad = lax.psum(out_grad, "seq").astype(F32)
    grad_weights = bmm(grad_heads, values, ((2,), (2,)))
    inner = jnp.sum(weights * grad_weights, axis=-1, keepdims=True)
    grad_scores = (weights * (grad_weights - inner)).astype(BF)
    grad_q = jnp.swapaxes(bmm(grad_scores, keys, ((2,), (1,))), 0, 1) * scale
    grad_k = jnp.swapaxes(bmm(grad_scores, queries, ((1,), (1,))), 0, 1) * scale
    grad_v = jnp.swapaxes(bmm(weights_low, grad_heads, ((1,), (1,))), 0, 1)
    grad_q_normed = rotate(grad_q, cosine, -sine)
    grad_k_normed = rotate(grad_k, cosine, -sine)
    q_gain_grad = jnp.sum(grad_q_normed * normed_q, axis=(0, 1))
    k_gain_grad = jnp.sum(grad_k_normed * normed_k, axis=(0, 1))
    grad_q_raw = norm_back(grad_q_normed * gain_query, normed_q, factor_q)
    grad_k_raw = norm_back(grad_k_normed * gain_key, normed_k, factor_k)
    grad_projected = (
        jnp.stack([grad_q_raw, grad_k_raw, grad_v], axis=1).reshape(length, cols).astype(BF)
    )
    qkv_grad = tn(hidden, grad_projected)
    grad_normed_part = nt(jnp.pad(grad_projected, ((0, 0), (0, LANES))), qkv_full)
    attn_gain_grad = jnp.sum(grad_normed_part * normed_all, axis=0)
    grad_normed_own = lax.psum_scatter(
        grad_normed_part.astype(BF), "seq", scatter_dimension=0, tiled=True
    ).astype(F32)
    normed_a, factor_a = normalize(inputs)
    tokens_grad = grad_residual + norm_back(grad_normed_own * gain_attn, normed_a, factor_a)

    def gain_column(vector):
        return jnp.pad(
            vector.reshape(wt_total, gain_part), ((0, 0), (0, shard - gain_part))
        ).reshape(model, 1)

    small_grad = jnp.concatenate(
        [
            router_grad,
            attn_gain_grad[:, None],
            ffn_gain_grad[:, None],
            gain_column(q_gain_grad),
            gain_column(k_gain_grad),
        ],
        axis=1,
    )
    small_grad = jnp.pad(small_grad, ((0, 0), (0, LANES - small_grad.shape[1])))
    scattered = lax.psum_scatter(
        jnp.concatenate([qkv_grad, small_grad], axis=1).astype(BF),
        "wt",
        scatter_dimension=0,
        tiled=True,
    )
    collected = lax.all_gather(scattered, "seq", axis=0).astype(F32)
    qkv_out = (
        collected[:, :, :cols]
        .reshape(seq_total, shard, 3, heads * HD)
        .transpose(1, 2, 0, 3)
        .reshape(shard, 3 * H * HD)
    )
    small_out = jnp.sum(collected[:, :, cols:], axis=0)
    return (
        output[None],
        tokens_grad[None],
        qkv_out,
        out_grad,
        small_out[:, :experts],
        gate_up_out,
        down_out,
        small_out[:, experts],
        small_out[:, experts + 1],
        small_out[:gain_part, experts + 2],
        small_out[:gain_part, experts + 3],
    )


def solution(mesh):
    in_specs = (
        P("wt", "seq", None),
        P("wt", "seq", None),
        P("wt", None),
        P("wt", "seq", None),
        P("wt", None),
        P("wt", None),
        P("wt", None),
        P("seq", "wt", None),
        P("seq", "wt", None),
        P("wt"),
        P("wt"),
        P("wt"),
        P("wt"),
    )
    out_specs = (
        P("wt", "seq", None),
        P("wt", "seq", None),
        P("wt", None),
        P("wt", None),
        P("wt", None),
        P("seq", "wt", None),
        P("seq", "wt", None),
        P("wt"),
        P("wt"),
        P("wt"),
        P("wt"),
    )
    return jax.shard_map(body, mesh=mesh, in_specs=in_specs, out_specs=out_specs, check_vma=False)
```

profile of v0, /device:TPU:0, one launch (start us, length us, event | category | flops | bytes accessed | tf_op | source)
XLA Modules:
  0.0 1457.3 jit_solution(14407658807051301885)
XLA Ops:
  18.4 39.6 %all-gather.25.cloned.1.call-done = bf16[1,512,2048]{2,1,0:T(8,128)(2,1)} async-done(((bf16[1,128,2048]{2,1,0:T(8,128)(2,1)}), bf16[1,512,2048]{2,1,0:T(8,128)(2,1)}) %all-gather.25.cloned.1.call-update) | async-done | bytes 2097168 | tf_op jit(solution)/shard_map/all_gather | solution.py:94
  60.1 48.1 %all-gather.19.cloned.1.call-done = bf16[2048,1664]{0,1:T(8,128)(2,1)} async-done(((bf16[256,1664]{0,1:T(8,128)(2,1)}), bf16[2048,1664]{0,1:T(8,128)(2,1)}) %all-gather.19.cloned.1.call-update) | async-done | bytes 6815760 | tf_op jit(solution)/shard_map/all_gather | solution.py:110
  110.0 8.6 fusion.3
  133.7 19.4 %all_to_all.33 = bf16[512,4,128]{2,1,0:T(4,128)(2,1)S(1)} all-to-all(bf16[512,4,128]{2,1,0:T(4,128)(2,1)S(1)} %copy.163), channel_id=1, replica_groups=mesh['seq'=4,'wt'=8] {'seq'}, dimensions={0} | all-to-all | bytes 1048576 | tf_op jit(solution)/shard_map/all_to_all | solution.py:148
  153.4 10.9 all-gather.21.cloned.1.call-done
  182.9 13.9 all-gather.1
  197.0 20.3 %all-gather.23.cloned.1.call-done = bf16[512,2048]{1,0:T(8,128)(2,1)} async-done(((bf16[128,2048]{1,0:T(8,128)(2,1)}), bf16[512,2048]{1,0:T(8,128)(2,1)}) %all-gather.23.cloned.1.call-update) | async-done | bytes 2097168 | tf_op jit(solution)/shard_map/all_gather | solution.py:155
  222.4 68.0 %all-gather.31.cloned.1.call-done = bf16[3072,2048]{1,0:T(8,128)(2,1)} async-done(((bf16[384,2048]{1,0:T(8,128)(2,1)}), bf16[3072,2048]{1,0:T(8,128)(2,1)}) %all-gather.31.cloned.1.call-update) | async-done | bytes 12582928 | tf_op jit(solution)/shard_map/all_gather | solution.py:114
  304.3 60.5 %all-gather.27.cloned.1.call-done = bf16[3072,2048]{1,0:T(8,128)(2,1)} async-done(((bf16[384,2048]{1,0:T(8,128)(2,1)}), bf16[3072,2048]{1,0:T(8,128)(2,1)}) %all-gather.27.cloned.1.call-update) | async-done | bytes 12582928 | tf_op jit(solution)/shard_map/all_gather | solution.py:114
  378.5 60.2 %all-gather.29.cloned.1.call-done = bf16[3072,2048]{1,0:T(8,128)(2,1)} async-done(((bf16[384,2048]{1,0:T(8,128)(2,1)}), bf16[3072,2048]{1,0:T(8,128)(2,1)}) %all-gather.29.cloned.1.call-update) | async-done | bytes 12582928 | tf_op jit(solution)/shard_map/all_gather | solution.py:114
  452.5 60.1 %all-gather.33.cloned.1.call-done = bf16[3072,2048]{1,0:T(8,128)(2,1)} async-done(((bf16[384,2048]{1,0:T(8,128)(2,1)}), bf16[3072,2048]{1,0:T(8,128)(2,1)}) %all-gather.33.cloned.1.call-update) | async-done | bytes 12582928 | tf_op jit(solution)/shard_map/all_gather | solution.py:114
  526.1 9.6 fusion.110
  559.9 9.1 multiply_convert_fusion.4
  583.8 10.7 fusion.39
  594.5 9.7 fusion.41
  611.5 12.3 add_convert_fusion
  642.1 30.1 %reduce-scatter.12.cloned.1.call-done = bf16[128,2080]{1,0:T(8,128)(2,1)} async-done(((bf16[512,2080]{1,0:T(8,128)(2,1)}), bf16[128,2080]{1,0:T(8,128)(2,1)}) %reduce-scatter.12.cloned.1.call-update) | async-done | bytes 532496 | tf_op jit(solution)/shard_map/reduce_scatter | solution.py:207
  677.6 40.4 %reduce-scatter.10.cloned.1.call-done = bf16[128,2048]{1,0:T(8,128)(2,1)} async-done(((bf16[512,2048]{1,0:T(8,128)(2,1)}), bf16[128,2048]{1,0:T(8,128)(2,1)}) %reduce-scatter.10.cloned.1.call-update) | async-done | bytes 524304 | tf_op jit(solution)/shard_map/reduce_scatter | solution.py:215
  737.4 14.1 all-to-all-done.1
  768.3 9.8 fusion.8
  806.8 9.1 pad_maximum_fusion.3
  826.3 9.1 pad_maximum_fusion.2
  845.9 9.1 pad_maximum_fusion.1
  865.3 9.0 pad_maximum_fusion
  875.6 35.4 %reduce-scatter.14.cloned.1.call-done = bf16[128,2048]{1,0:T(8,128)(2,1)} async-done(((bf16[512,2048]{1,0:T(8,128)(2,1)}), bf16[128,2048]{1,0:T(8,128)(2,1)}) %reduce-scatter.14.cloned.1.call-update) | async-done | bytes 524304 | tf_op jit(solution)/shard_map/reduce_scatter | solution.py:262
  914.8 49.5 %all-reduce.9.cloned.1.call-done = bf16[256,2048]{1,0:T(8,128)(2,1)} async-done(((bf16[256,2048]{1,0:T(8,128)(2,1)}), bf16[256,2048]{1,0:T(8,128)(2,1)}) %all-reduce.9.cloned.1.call-update) | async-done | bytes 1048592 | tf_op jit(solution)/shard_map/psum | solution.py:243
  967.1 92.2 %reduce-scatter.26.cloned.1.call-done = bf16[1,384,2048]{2,1,0:T(8,128)(2,1)} async-done(((bf16[8,384,2048]{2,1,0:T(8,128)(2,1)}), bf16[1,384,2048]{2,1,0:T(8,128)(2,1)}) %reduce-scatter.26.cloned.1.call-update) | async-done | bytes 1572880 | tf_op jit(solution)/shard_map/reduce_scatter | solution.py:196
  1061.1 93.8 %reduce-scatter.24.cloned.1.call-done = bf16[1,384,2048]{2,1,0:T(8,128)(2,1)} async-done(((bf16[8,384,2048]{2,1,0:T(8,128)(2,1)}), bf16[1,384,2048]{2,1,0:T(8,128)(2,1)}) %reduce-scatter.24.cloned.1.call-update) | async-done | bytes 1572880 | tf_op jit(solution)/shard_map/reduce_scatter | solution.py:196
  1158.9 91.7 %reduce-scatter.22.cloned.1.call-done = bf16[1,384,2048]{2,1,0:T(8,128)(2,1)} async-done(((bf16[8,384,2048]{2,1,0:T(8,128)(2,1)}), bf16[1,384,2048]{2,1,0:T(8,128)(2,1)}) %reduce-scatter.22.cloned.1.call-update) | async-done | bytes 1572880 | tf_op jit(solution)/shard_map/reduce_scatter | solution.py:196
  1254.6 91.8 %reduce-scatter.20.cloned.1.call-done = bf16[1,384,2048]{2,1,0:T(8,128)(2,1)} async-done(((bf16[8,384,2048]{2,1,0:T(8,128)(2,1)}), bf16[1,384,2048]{2,1,0:T(8,128)(2,1)}) %reduce-scatter.20.cloned.1.call-update) | async-done | bytes 1572880 | tf_op jit(solution)/shard_map/reduce_scatter | solution.py:196
  1356.2 59.4 %all-gather.37.cloned.1.call-done = bf16[1024,1664]{0,1:T(8,128)(2,1)} async-done(((bf16[256,1664]{0,1:T(8,128)(2,1)}), bf16[1024,1664]{0,1:T(8,128)(2,1)}) %all-gather.37.cloned.1.call-update) | async-done | bytes 3407888 | tf_op jit(solution)/shard_map/all_gather | solution.py:290
  1433.3 8.7 copy.187
  (411 shorter events, 327.3 us)
Async XLA Ops:
  7.2 50.8 %all-gather.25.cloned.1.call-start = ((), (), s32[]{:S(2)}) async-start(), calls=%async_computation.24 | async-start | bytes 2621440 | tf_op jit(solution)/shard_map/all_gather | solution.py:94
  7.9 100.2 %all-gather.19.cloned.1.call-start = ((), (), s32[]{:S(2)}) async-start(), calls=%async_computation.11 | async-start | bytes 7667712 | tf_op jit(solution)/shard_map/all_gather | solution.py:110
  13.8 94.4 %copy-start.73 = (bf16[8,128]{1,0:T(8,128)(2,1)S(1)}, bf16[8,128]{1,0:T(8,128)(2,1)}, u32[]{:S(2)}) copy-start(bf16[8,128]{1,0:T(8,128)(2,1)} %constant.61.clone) | copy-start | bytes 6148
  14.9 149.4 %all-gather.21.cloned.1.call-start = ((), (), s32[]{:S(2)}) async-start(), calls=%async_computation.12 | async-start | bytes 9437184 | tf_op jit(solution)/shard_map/all_gather | solution.py:111
  15.7 201.6 %all-gather.23.cloned.1.call-start = ((), (), s32[]{:S(2)}) async-start(), calls=%async_computation.13 | async-start | bytes 2621440 | tf_op jit(solution)/shard_map/all_gather | solution.py:155
  18.4 106.9 %copy-start.28 = (f32[512,64]{1,0:T(8,128)}, f32[512,64]{1,0:T(8,128)S(1)}, u32[]{:S(2)}) copy-start(f32[512,64]{1,0:T(8,128)S(1)} %get-tuple-element.77) | copy-start | bytes 393220
  60.1 49.4 %copy-start.74 = (f32[512]{0:T(512)}, f32[512]{0:T(512)S(1)}, u32[]{:S(2)}) copy-start(f32[512]{0:T(512)S(1)} %add_rsqrt_fusion.2) | copy-start | bytes 6148
  109.5 59.8 %copy-start.53 = (f32[1,2048]{1,0:T(1,128)}, f32[1,2048]{1,0:T(1,128)S(1)}, u32[]{:S(2)}) copy-start(f32[1,2048]{1,0:T(1,128)S(1)} %get-tuple-element.73) | copy-start | bytes 24580
  171.2 119.2 %all-gather.31.cloned.1.call-start = ((), (), s32[]{:S(2)}) async-start(), calls=%async_computation.27 | async-start | bytes 14155776 | tf_op jit(solution)/shard_map/all_gather | solution.py:114
  175.8 189.0 %all-gather.27.cloned.1.call-start = ((), (), s32[]{:S(2)}) async-start(), calls=%async_computation.25 | async-start | bytes 14155776 | tf_op jit(solution)/shard_map/all_gather | solution.py:114
  178.2 260.5 %all-gather.29.cloned.1.call-start = ((), (), s32[]{:S(2)}) async-start(), calls=%async_computation.26 | async-start | bytes 14155776 | tf_op jit(solution)/shard_map/all_gather | solution.py:114
  180.8 331.8 %all-gather.33.cloned.1.call-start = ((), (), s32[]{:S(2)}) async-start(), calls=%async_computation.28 | async-start | bytes 14155776 | tf_op jit(solution)/shard_map/all_gather | solution.py:114
  182.1 377.8 %all-gather.35.cloned.1.call-start = ((), (), s32[]{:S(2)}) async-start(), calls=%async_computation.29 | async-start | bytes 2621440 | tf_op jit(solution)/shard_map/all_gather | solution.py:112
  182.8 489.3 %reduce-scatter.12.cloned.1.call-start = ((), (), s32[]{:S(2)}) async-start(), calls=%async_computation.15 | async-start | bytes 2785280 | tf_op jit(solution)/shard_map/reduce_scatter | solution.py:207
  197.0 101.9 %copy-start.49 = (pred[512,16]{1,0:T(8,128)(4,1)}, pred[512,16]{1,0:T(8,128)(4,1)S(1)}, u32[]{:S(2)}) copy-start(pred[512,16]{1,0:T(8,128)(4,1)S(1)} %copy.167) | copy-start | bytes 24580
  220.2 78.6 %copy-start.64 = (f32[512]{0:T(512)}, f32[512]{0:T(512)S(1)}, u32[]{:S(2)}) copy-start(f32[512]{0:T(512)S(1)} %get-tuple-element.25) | copy-start | bytes 6148
  583.2 53.8 %copy-start.78 = (bf16[512,1024]{1,0:T(8,128)(2,1)}, bf16[512,1024]{1,0:T(8,128)(2,1)S(1)}, u32[]{:S(2)}) copy-start(bf16[512,1024]{1,0:T(8,128)(2,1)S(1)} %get-tuple-element.39) | copy-start | bytes 3145732
  626.7 91.3 %reduce-scatter.10.cloned.1.call-start = ((), (), s32[]{:S(2)}) async-start(), calls=%async_computation.14 | async-start | bytes 2621440 | tf_op jit(solution)/shard_map/reduce_scatter | solution.py:215
  637.0 37.4 %copy-start.46 = (f32[512,16]{1,0:T(8,128)S(1)}, f32[512,16]{1,0:T(8,128)}, u32[]{:S(2)}) copy-start(f32[512,16]{1,0:T(8,128)} %copy-done.45) | copy-start | bytes 98308
  640.8 34.6 %copy-start.71 = (f32[128]{0:T(128)S(1)}, f32[128]{0:T(128)}, u32[]{:S(2)}) copy-start(f32[128]{0:T(128)} %copy-done.70) | copy-start | bytes 1540
  640.8 77.2 %copy-start.35 = (bf16[1,128,2048]{2,1,0:T(8,128)(2,1)S(1)}, bf16[1,128,2048]{2,1,0:T(8,128)(2,1)}, u32[]{:S(2)}) copy-start(bf16[1,128,2048]{2,1,0:T(8,128)(2,1)} %param.15) | copy-start | bytes 1572868
  640.9 156.3 %reduce-scatter.18.cloned.1.call-start = ((), (), s32[]{:S(2)}) async-start(), calls=%async_computation.18 | async-start | bytes 9437184 | tf_op jit(solution)/shard_map/reduce_scatter | solution.py:240
  674.3 46.2 %copy-start.9 = (bf16[128,4,4,128]{0,3,2,1:T(8,128)(2,1)S(1)}, bf16[128,4,4,128]{0,3,2,1:T(8,128)(2,1)}, u32[]{:S(2)}) copy-start(bf16[128,4,4,128]{0,3,2,1:T(8,128)(2,1)} %copy-done.8) | copy-start | bytes 1572868
  733.6 17.9 %all-to-all-start.1 = ((bf16[128,16,128]{2,0,1:T(8,128)(2,1)}), bf16[128,16,128]{2,0,1:T(8,128)(2,1)S(1)}, u32[]{:S(2)}, u32[]{:S(2)}) async-start(bf16[128,16,128]{2,0,1:T(8,128)(2,1)} %bitcast.275), calls=%async_computation.3 | async-start | bytes 1048576 | tf_op jit(solution)/shard_map/all_to_all | solution.py:238
  737.1 137.4 %reduce-scatter.16.cloned.1.call-start = ((), (), s32[]{:S(2)}) async-start(), calls=%async_computation.17 | async-start | bytes 7667712 | tf_op jit(solution)/shard_map/reduce_scatter | solution.py:284
  791.9 119.1 %reduce-scatter.14.cloned.1.call-start = ((), (), s32[]{:S(2)}) async-start(), calls=%async_computation.16 | async-start | bytes 2621440 | tf_op jit(solution)/shard_map/reduce_scatter | solution.py:262
  792.5 171.9 %all-reduce.9.cloned.1.call-start = ((), (), s32[]{:S(2)}) async-start(), calls=%async_computation.19 | async-start | bytes 2097152 | tf_op jit(solution)/shard_map/psum | solution.py:243
  797.2 262.1 %reduce-scatter.26.cloned.1.call-start = ((), (), s32[]{:S(2)}) async-start(), calls=%async_computation.23 | async-start | bytes 14155776 | tf_op jit(solution)/shard_map/reduce_scatter | solution.py:196
  815.9 339.1 %reduce-scatter.24.cloned.1.call-start = ((), (), s32[]{:S(2)}) async-start(), calls=%async_computation.22 | async-start | bytes 14155776 | tf_op jit(solution)/shard_map/reduce_scatter | solution.py:196
  835.4 415.2 %reduce-scatter.22.cloned.1.call-start = ((), (), s32[]{:S(2)}) async-start(), calls=%async_computation.21 | async-start | bytes 14155776 | tf_op jit(solution)/shard_map/reduce_scatter | solution.py:196
  855.0 491.5 %reduce-scatter.20.cloned.1.call-start = ((), (), s32[]{:S(2)}) async-start(), calls=%async_computation.20 | async-start | bytes 14155776 | tf_op jit(solution)/shard_map/reduce_scatter | solution.py:196
  874.4 541.2 %all-gather.37.cloned.1.call-start = ((), (), s32[]{:S(2)}) async-start(), calls=%async_computation.30 | async-start | bytes 4259840 | tf_op jit(solution)/shard_map/all_gather | solution.py:290
  (95 other events, 575.3 us)
Sparse Core Ops, SparseCore 0:
  9.6 48.3 all-gather.24
  60.4 47.6 all-gather.18
  110.1 54.2 all-gather.20
  171.3 45.9 all-gather.22
  219.6 70.7 all-gather.30
  292.7 71.9 all-gather.26
  366.7 71.9 all-gather.28
  440.6 71.9 all-gather.32
  514.2 45.6 all-gather.34
  626.8 45.2 reduce-scatter.11
  675.0 42.9 reduce-scatter.9
  726.4 70.6 reduce-scatter.17
  800.6 64.0 reduce-scatter.15
  867.4 43.6 reduce-scatter.13
  913.2 51.0 all-reduce.8
  967.7 91.5 reduce-scatter.25
  1062.6 92.2 reduce-scatter.23
  1158.3 92.2 reduce-scatter.21
  1254.1 92.2 reduce-scatter.19
  1347.9 67.6 all-gather.36
where the time goes:
time: 1470 us; the launch traced here: 1460 us
  waiting for transfers between devices  979 us (67%)
  matrix products  200 us (14%)
  local copies, waits for them, and re-layouts  134 us (9%)
  other arithmetic  88.7 us (6%)
  blocking collectives  33.2 us (2%)
  between operations  16 us (1%)
    reduce_scatter x4, waiting for transfers between devices, body(): lax.psum_scatter(joined, 'wt', scatter_dimension=0, tiled=False).astype(F32)  369 us
    all_gather x4, waiting for transfers between devices, body(): lax.all_gather(jnp.concatenate([w_gate_up[e], w_down[e]], axis=0), 'wt',...  249 us
    dot_general x34, matrix products, dot(): lax.dot_general(left, right, (dims, ((), ())), preferred_element_type=F32)  188 us
    all_gather x1, waiting for transfers between devices, body(): collected = lax.all_gather(scattered, 'seq', axis=0).astype(F32)  59.4 us
    psum x1, waiting for transfers between devices, body(): out_grad = lax.psum(out_grad, 'seq').astype(F32)  49.5 us
    all_gather x1, waiting for transfers between devices, body(): lax.all_gather(jnp.concatenate([w_here, small], axis=1), 'wt', axis=0, ti...  48.1 us
    reduce_scatter x1, waiting for transfers between devices, body(): lax.psum_scatter(out_part.astype(BF), 'seq', scatter_dimension=0, tiled=T...  40.4 us
    all_gather x1, waiting for transfers between devices, body(): tokens_all = lax.all_gather(tokens[0], 'seq', axis=0, tiled=True)  39.6 us
  transfers between devices with their start and end apart: 21, of which 20 were waited for; matrix products, arithmetic and copies ran while one was open for 20% of the time, Pallas kernels for 0%

commit v1 on v0

--- a/solution.py
+++ b/solution.py
@@ -240,7 +240,11 @@
     out_grad = lax.psum_scatter(
         tn(merged, grad_branch).astype(BF), "wt", scatter_dimension=0, tiled=True
     )
-    out_grad = lax.psum(out_grad, "seq").astype(F32)
+
+    def note_the_slabs(local, along_axis):
+        return lax.all_gather(local, along_axis).sum(axis=0)
+
+    out_grad = note_the_slabs(out_grad, "seq").astype(F32)
     grad_weights = bmm(grad_heads, values, ((2,), (2,)))
     inner = jnp.sum(weights * grad_weights, axis=-1, keepdims=True)
     grad_scores = (weights * (grad_weights - inner)).astype(BF)

time: 1470 us -> 1520 us (1.034)
  waiting for transfers between devices: 979 us -> 1030 us
    psum x1 -> x0, waiting for transfers between devices: 49.5 us -> none  [body(): out_grad = lax.psum(out_grad, 'seq').astype(F32)]
    reduce_scatter x1, waiting for transfers between devices: 4.6 us -> 52 us  [body(): lax.psum_scatter(tn(merged, grad_branch).astype(BF), 'wt', scatter_dimens...]
    all_gather x0 -> x1, waiting for transfers between devices: none -> 45.6 us  [note_the_slabs(): return lax.all_gather(local, along_axis).sum(axis=0)]
  transfers between devices with their start and end apart: 21 -> 21, of which waited for: 20 -> 20; matrix products, arithmetic and copies ran while one was open for 20% -> 19% of each run, Pallas kernels for 0% -> 0%
where the time goes in v1:
time: 1520 us; the launch traced here: 1510 us
  waiting for transfers between devices  1030 us (68%)
  matrix products  200 us (13%)
  local copies, waits for them, and re-layouts  135 us (9%)
  other arithmetic  90.5 us (6%)
  blocking collectives  33.2 us (2%)
  between operations  16 us (1%)
    reduce_scatter x4, waiting for transfers between devices, body(): lax.psum_scatter(joined, 'wt', scatter_dimension=0, tiled=False).astype(F32)  368 us
    all_gather x4, waiting for transfers between devices, body(): lax.all_gather(jnp.concatenate([w_gate_up[e], w_down[e]], axis=0), 'wt',...  249 us
    dot_general x34, matrix products, dot(): lax.dot_general(left, right, (dims, ((), ())), preferred_element_type=F32)  187 us
    all_gather x1, waiting for transfers between devices, body(): collected = lax.all_gather(scattered, 'seq', axis=0).astype(F32)  59.6 us
    reduce_scatter x1, waiting for transfers between devices, body(): lax.psum_scatter(tn(merged, grad_branch).astype(BF), 'wt', scatter_dimens...  52 us
    all_gather x1, waiting for transfers between devices, body(): lax.all_gather(jnp.concatenate([w_here, small], axis=1), 'wt', axis=0, ti...  48.1 us
    reduce_scatter x1, waiting for transfers between devices, body(): lax.psum_scatter(grad_normed_part.astype(BF), 'seq', scatter_dimension=0,...  46.1 us
    all_gather x1, waiting for transfers between devices, note_the_slabs(): return lax.all_gather(local, along_axis).sum(axis=0)  45.6 us
  transfers between devices with their start and end apart: 21, of which 20 were waited for; matrix products, arithmetic and copies ran while one was open for 19% of the time, Pallas kernels for 0%

profile of v1, /device:TPU:0, one launch (start us, length us, event | category | flops | bytes accessed | tf_op | source)
XLA Modules:
  0.0 1514.1 jit_solution(11690220598688854822)
XLA Ops:
  18.4 39.6 %all-gather.27.cloned.1.call-done = bf16[1,512,2048]{2,1,0:T(8,128)(2,1)} async-done(((bf16[1,128,2048]{2,1,0:T(8,128)(2,1)}), bf16[1,512,2048]{2,1,0:T(8,128)(2,1)}) %all-gather.27.cloned.1.call-update) | async-done | bytes 2097168 | tf_op jit(solution)/shard_map/all_gather | solution.py:94
  60.1 48.1 %all-gather.21.cloned.1.call-done = bf16[2048,1664]{0,1:T(8,128)(2,1)} async-done(((bf16[256,1664]{0,1:T(8,128)(2,1)}), bf16[2048,1664]{0,1:T(8,128)(2,1)}) %all-gather.21.cloned.1.call-update) | async-done | bytes 6815760 | tf_op jit(solution)/shard_map/all_gather | solution.py:110
  110.0 8.6 fusion.3
  133.8 19.4 %all_to_all.33 = bf16[512,4,128]{2,1,0:T(4,128)(2,1)S(1)} all-to-all(bf16[512,4,128]{2,1,0:T(4,128)(2,1)S(1)} %copy.163), channel_id=1, replica_groups=mesh['seq'=4,'wt'=8] {'seq'}, dimensions={0} | all-to-all | bytes 1048576 | tf_op jit(solution)/shard_map/all_to_all | solution.py:148
  153.5 10.9 all-gather.23.cloned.1.call-done
  182.9 13.9 all-gather.1
  197.0 20.3 %all-gather.25.cloned.1.call-done = bf16[512,2048]{1,0:T(8,128)(2,1)} async-done(((bf16[128,2048]{1,0:T(8,128)(2,1)}), bf16[512,2048]{1,0:T(8,128)(2,1)}) %all-gather.25.cloned.1.call-update) | async-done | bytes 2097168 | tf_op jit(solution)/shard_map/all_gather | solution.py:155
  222.5 68.0 %all-gather.33.cloned.1.call-done = bf16[3072,2048]{1,0:T(8,128)(2,1)} async-done(((bf16[384,2048]{1,0:T(8,128)(2,1)}), bf16[3072,2048]{1,0:T(8,128)(2,1)}) %all-gather.33.cloned.1.call-update) | async-done | bytes 12582928 | tf_op jit(solution)/shard_map/all_gather | solution.py:114
  304.3 60.5 %all-gather.29.cloned.1.call-done = bf16[3072,2048]{1,0:T(8,128)(2,1)} async-done(((bf16[384,2048]{1,0:T(8,128)(2,1)}), bf16[3072,2048]{1,0:T(8,128)(2,1)}) %all-gather.29.cloned.1.call-update) | async-done | bytes 12582928 | tf_op jit(solution)/shard_map/all_gather | solution.py:114
  378.5 60.2 %all-gather.31.cloned.1.call-done = bf16[3072,2048]{1,0:T(8,128)(2,1)} async-done(((bf16[384,2048]{1,0:T(8,128)(2,1)}), bf16[3072,2048]{1,0:T(8,128)(2,1)}) %all-gather.31.cloned.1.call-update) | async-done | bytes 12582928 | tf_op jit(solution)/shard_map/all_gather | solution.py:114
  452.5 60.1 %all-gather.35.cloned.1.call-done = bf16[3072,2048]{1,0:T(8,128)(2,1)} async-done(((bf16[384,2048]{1,0:T(8,128)(2,1)}), bf16[3072,2048]{1,0:T(8,128)(2,1)}) %all-gather.35.cloned.1.call-update) | async-done | bytes 12582928 | tf_op jit(solution)/shard_map/all_gather | solution.py:114
  526.1 9.6 fusion.110
  559.9 9.1 multiply_convert_fusion.4
  583.8 10.7 fusion.39
  594.6 9.7 fusion.41
  611.4 12.3 add_convert_fusion
  641.7 30.3 %reduce-scatter.12.cloned.1.call-done = bf16[128,2080]{1,0:T(8,128)(2,1)} async-done(((bf16[512,2080]{1,0:T(8,128)(2,1)}), bf16[128,2080]{1,0:T(8,128)(2,1)}) %reduce-scatter.12.cloned.1.call-update) | async-done | bytes 532496 | tf_op jit(solution)/shard_map/reduce_scatter | solution.py:207
  676.6 41.3 %reduce-scatter.10.cloned.1.call-done = bf16[128,2048]{1,0:T(8,128)(2,1)} async-done(((bf16[512,2048]{1,0:T(8,128)(2,1)}), bf16[128,2048]{1,0:T(8,128)(2,1)}) %reduce-scatter.10.cloned.1.call-update) | async-done | bytes 524304 | tf_op jit(solution)/shard_map/reduce_scatter | solution.py:215
  731.7 13.6 all-to-all-done.1
  762.1 9.6 fusion.8
  803.9 9.1 pad_maximum_fusion.3
  823.4 9.2 pad_maximum_fusion.2
  842.9 9.1 pad_maximum_fusion.1
  862.4 9.0 pad_maximum_fusion
  872.5 52.0 %reduce-scatter.18.cloned.1.call-done = bf16[256,2048]{1,0:T(8,128)(2,1)} async-done(((bf16[2048,2048]{1,0:T(8,128)(2,1)}), bf16[256,2048]{1,0:T(8,128)(2,1)}) %reduce-scatter.18.cloned.1.call-update) | async-done | bytes 1048592 | tf_op jit(solution)/shard_map/reduce_scatter | solution.py:240
  924.7 46.1 %reduce-scatter.14.cloned.1.call-done = bf16[128,2048]{1,0:T(8,128)(2,1)} async-done(((bf16[512,2048]{1,0:T(8,128)(2,1)}), bf16[128,2048]{1,0:T(8,128)(2,1)}) %reduce-scatter.14.cloned.1.call-update) | async-done | bytes 524304 | tf_op jit(solution)/shard_map/reduce_scatter | solution.py:266
  974.6 91.1 %reduce-scatter.26.cloned.1.call-done = bf16[1,384,2048]{2,1,0:T(8,128)(2,1)} async-done(((bf16[8,384,2048]{2,1,0:T(8,128)(2,1)}), bf16[1,384,2048]{2,1,0:T(8,128)(2,1)}) %reduce-scatter.26.cloned.1.call-update) | async-done | bytes 1572880 | tf_op jit(solution)/shard_map/reduce_scatter | solution.py:196
  1067.5 93.8 %reduce-scatter.24.cloned.1.call-done = bf16[1,384,2048]{2,1,0:T(8,128)(2,1)} async-done(((bf16[8,384,2048]{2,1,0:T(8,128)(2,1)}), bf16[1,384,2048]{2,1,0:T(8,128)(2,1)}) %reduce-scatter.24.cloned.1.call-update) | async-done | bytes 1572880 | tf_op jit(solution)/shard_map/reduce_scatter | solution.py:196
  1165.4 91.7 %reduce-scatter.22.cloned.1.call-done = bf16[1,384,2048]{2,1,0:T(8,128)(2,1)} async-done(((bf16[8,384,2048]{2,1,0:T(8,128)(2,1)}), bf16[1,384,2048]{2,1,0:T(8,128)(2,1)}) %reduce-scatter.22.cloned.1.call-update) | async-done | bytes 1572880 | tf_op jit(solution)/shard_map/reduce_scatter | solution.py:196
  1261.0 91.7 %reduce-scatter.20.cloned.1.call-done = bf16[1,384,2048]{2,1,0:T(8,128)(2,1)} async-done(((bf16[8,384,2048]{2,1,0:T(8,128)(2,1)}), bf16[1,384,2048]{2,1,0:T(8,128)(2,1)}) %reduce-scatter.20.cloned.1.call-update) | async-done | bytes 1572880 | tf_op jit(solution)/shard_map/reduce_scatter | solution.py:196
  1362.5 59.6 %all-gather.39.cloned.1.call-done = bf16[1024,1664]{0,1:T(8,128)(2,1)} async-done(((bf16[256,1664]{0,1:T(8,128)(2,1)}), bf16[1024,1664]{0,1:T(8,128)(2,1)}) %all-gather.39.cloned.1.call-update) | async-done | bytes 3407888 | tf_op jit(solution)/shard_map/all_gather | solution.py:294
  1456.8 45.6 %all-gather.41.cloned.1.call-done = bf16[1024,2048]{1,0:T(8,128)(2,1)} async-done(((bf16[256,2048]{1,0:T(8,128)(2,1)}), bf16[1024,2048]{1,0:T(8,128)(2,1)}) %all-gather.41.cloned.1.call-update) | async-done | bytes 4194320 | tf_op jit(solution)/shard_map/all_gather | solution.py:245
  (414 shorter events, 334.3 us)
Async XLA Ops:
  7.2 50.8 %all-gather.27.cloned.1.call-start = ((), (), s32[]{:S(2)}) async-start(), calls=%async_computation.23 | async-start | bytes 2621440 | tf_op jit(solution)/shard_map/all_gather | solution.py:94
  7.9 100.2 %all-gather.21.cloned.1.call-start = ((), (), s32[]{:S(2)}) async-start(), calls=%async_computation.11 | async-start | bytes 7667712 | tf_op jit(solution)/shard_map/all_gather | solution.py:110
  13.8 94.4 %copy-start.73 = (bf16[8,128]{1,0:T(8,128)(2,1)S(1)}, bf16[8,128]{1,0:T(8,128)(2,1)}, u32[]{:S(2)}) copy-start(bf16[8,128]{1,0:T(8,128)(2,1)} %constant.62.clone) | copy-start | bytes 6148
  14.9 149.4 %all-gather.23.cloned.1.call-start = ((), (), s32[]{:S(2)}) async-start(), calls=%async_computation.12 | async-start | bytes 9437184 | tf_op jit(solution)/shard_map/all_gather | solution.py:111
  15.7 201.7 %all-gather.25.cloned.1.call-start = ((), (), s32[]{:S(2)}) async-start(), calls=%async_computation.13 | async-start | bytes 2621440 | tf_op jit(solution)/shard_map/all_gather | solution.py:155
  18.4 106.9 %copy-start.28 = (f32[512,64]{1,0:T(8,128)}, f32[512,64]{1,0:T(8,128)S(1)}, u32[]{:S(2)}) copy-start(f32[512,64]{1,0:T(8,128)S(1)} %get-tuple-element.77) | copy-start | bytes 393220
  60.1 49.4 %copy-start.74 = (f32[512]{0:T(512)}, f32[512]{0:T(512)S(1)}, u32[]{:S(2)}) copy-start(f32[512]{0:T(512)S(1)} %add_rsqrt_fusion.2) | copy-start | bytes 6148
  109.5 59.8 %copy-start.53 = (f32[1,2048]{1,0:T(1,128)}, f32[1,2048]{1,0:T(1,128)S(1)}, u32[]{:S(2)}) copy-start(f32[1,2048]{1,0:T(1,128)S(1)} %get-tuple-element.73) | copy-start | bytes 24580
  171.2 119.2 %all-gather.33.cloned.1.call-start = ((), (), s32[]{:S(2)}) async-start(), calls=%async_computation.26 | async-start | bytes 14155776 | tf_op jit(solution)/shard_map/all_gather | solution.py:114
  175.8 189.0 %all-gather.29.cloned.1.call-start = ((), (), s32[]{:S(2)}) async-start(), calls=%async_computation.24 | async-start | bytes 14155776 | tf_op jit(solution)/shard_map/all_gather | solution.py:114
  178.2 260.5 %all-gather.31.cloned.1.call-start = ((), (), s32[]{:S(2)}) async-start(), calls=%async_computation.25 | async-start | bytes 14155776 | tf_op jit(solution)/shard_map/all_gather | solution.py:114
  180.8 331.8 %all-gather.35.cloned.1.call-start = ((), (), s32[]{:S(2)}) async-start(), calls=%async_computation.27 | async-start | bytes 14155776 | tf_op jit(solution)/shard_map/all_gather | solution.py:114
  182.1 377.8 %all-gather.37.cloned.1.call-start = ((), (), s32[]{:S(2)}) async-start(), calls=%async_computation.28 | async-start | bytes 2621440 | tf_op jit(solution)/shard_map/all_gather | solution.py:112
  182.9 489.2 %reduce-scatter.12.cloned.1.call-start = ((), (), s32[]{:S(2)}) async-start(), calls=%async_computation.15 | async-start | bytes 2785280 | tf_op jit(solution)/shard_map/reduce_scatter | solution.py:207
  197.0 101.9 %copy-start.49 = (pred[512,16]{1,0:T(8,128)(4,1)}, pred[512,16]{1,0:T(8,128)(4,1)S(1)}, u32[]{:S(2)}) copy-start(pred[512,16]{1,0:T(8,128)(4,1)S(1)} %copy.167) | copy-start | bytes 24580
  220.3 78.6 %copy-start.64 = (f32[512]{0:T(512)}, f32[512]{0:T(512)S(1)}, u32[]{:S(2)}) copy-start(f32[512]{0:T(512)S(1)} %get-tuple-element.25) | copy-start | bytes 6148
  583.3 53.7 %copy-start.77 = (bf16[512,1024]{1,0:T(8,128)(2,1)}, bf16[512,1024]{1,0:T(8,128)(2,1)S(1)}, u32[]{:S(2)}) copy-start(bf16[512,1024]{1,0:T(8,128)(2,1)S(1)} %get-tuple-element.39) | copy-start | bytes 3145732
  626.6 91.3 %reduce-scatter.10.cloned.1.call-start = ((), (), s32[]{:S(2)}) async-start(), calls=%async_computation.14 | async-start | bytes 2621440 | tf_op jit(solution)/shard_map/reduce_scatter | solution.py:215
  637.0 37.2 %copy-start.46 = (f32[512,16]{1,0:T(8,128)S(1)}, f32[512,16]{1,0:T(8,128)}, u32[]{:S(2)}) copy-start(f32[512,16]{1,0:T(8,128)} %copy-done.45) | copy-start | bytes 98308
  640.8 34.4 %copy-start.54 = (f32[1,2048]{1,0:T(1,128)S(1)}, f32[1,2048]{1,0:T(1,128)}, u32[]{:S(2)}) copy-start(f32[1,2048]{1,0:T(1,128)} %copy-done.53) | copy-start | bytes 24580
  640.8 34.4 %copy-start.71 = (f32[128]{0:T(128)S(1)}, f32[128]{0:T(128)}, u32[]{:S(2)}) copy-start(f32[128]{0:T(128)} %copy-done.70) | copy-start | bytes 1540
  727.5 17.8 %all-to-all-start.1 = ((bf16[128,16,128]{2,0,1:T(8,128)(2,1)}), bf16[128,16,128]{2,0,1:T(8,128)(2,1)S(1)}, u32[]{:S(2)}, u32[]{:S(2)}) async-start(bf16[128,16,128]{2,0,1:T(8,128)(2,1)} %bitcast.276), calls=%async_computation.3 | async-start | bytes 1048576 | tf_op jit(solution)/shard_map/all_to_all | solution.py:238
  731.0 140.6 %reduce-scatter.16.cloned.1.call-start = ((), (), s32[]{:S(2)}) async-start(), calls=%async_computation.17 | async-start | bytes 7667712 | tf_op jit(solution)/shard_map/reduce_scatter | solution.py:288
  785.6 138.9 %reduce-scatter.18.cloned.1.call-start = ((), (), s32[]{:S(2)}) async-start(), calls=%async_computation.18 | async-start | bytes 9437184 | tf_op jit(solution)/shard_map/reduce_scatter | solution.py:240
  793.0 177.9 %reduce-scatter.14.cloned.1.call-start = ((), (), s32[]{:S(2)}) async-start(), calls=%async_computation.16 | async-start | bytes 2621440 | tf_op jit(solution)/shard_map/reduce_scatter | solution.py:266
  793.6 272.1 %reduce-scatter.26.cloned.1.call-start = ((), (), s32[]{:S(2)}) async-start(), calls=%async_computation.22 | async-start | bytes 14155776 | tf_op jit(solution)/shard_map/reduce_scatter | solution.py:196
  813.0 348.4 %reduce-scatter.24.cloned.1.call-start = ((), (), s32[]{:S(2)}) async-start(), calls=%async_computation.21 | async-start | bytes 14155776 | tf_op jit(solution)/shard_map/reduce_scatter | solution.py:196
  832.6 424.5 %reduce-scatter.22.cloned.1.call-start = ((), (), s32[]{:S(2)}) async-start(), calls=%async_computation.20 | async-start | bytes 14155776 | tf_op jit(solution)/shard_map/reduce_scatter | solution.py:196
  852.1 500.7 %reduce-scatter.20.cloned.1.call-start = ((), (), s32[]{:S(2)}) async-start(), calls=%async_computation.19 | async-start | bytes 14155776 | tf_op jit(solution)/shard_map/reduce_scatter | solution.py:196
  871.5 53.1 %copy-start.7 = (bf16[1,128,2048]{2,1,0:T(8,128)(2,1)S(1)}, bf16[1,128,2048]{2,1,0:T(8,128)(2,1)}, u32[]{:S(2)}) copy-start(bf16[1,128,2048]{2,1,0:T(8,128)(2,1)} %param.14) | copy-start | bytes 1572868
  871.5 550.5 %all-gather.39.cloned.1.call-start = ((), (), s32[]{:S(2)}) async-start(), calls=%async_computation.29 | async-start | bytes 4259840 | tf_op jit(solution)/shard_map/all_gather | solution.py:294
  872.2 630.1 %all-gather.41.cloned.1.call-start = ((), (), s32[]{:S(2)}) async-start(), calls=%async_computation.30 | async-start | bytes 5242880 | tf_op jit(solution)/shard_map/all_gather | solution.py:245
  (96 other events, 519.4 us)
Sparse Core Ops, SparseCore 0:
  9.6 48.3 all-gather.26
  60.4 47.6 all-gather.20
  110.1 54.2 all-gather.22
  171.4 45.9 all-gather.24
  219.6 70.7 all-gather.32
  292.8 71.9 all-gather.28
  366.7 71.9 all-gather.30
  440.6 71.9 all-gather.34
  514.2 45.6 all-gather.36
  626.7 45.2 reduce-scatter.11
  674.9 42.9 reduce-scatter.9
  785.8 63.1 reduce-scatter.15
  852.9 71.5 reduce-scatter.17
  927.2 43.5 reduce-scatter.13
  974.2 91.4 reduce-scatter.25
  1069.1 92.2 reduce-scatter.23
  1164.7 92.2 reduce-scatter.21
  1260.4 92.2 reduce-scatter.19
  1354.3 67.6 all-gather.38
  1423.4 78.9 all-gather.40
